TPU v7x, 8 devices: a whole 2x2x1 slice. The times are simulated.
8 devices in a mesh: data: 4 (over z, y, x), stage: 2 (over core).
Axes of the slice: x: 2, y: 2, z: 1, core: 2. Of those that a mesh axis runs over, the one named last changes fastest.
Arguments:
- master_up: float32 [2, 896, 4864], P('stage', 'data')
- master_down: float32 [2, 4864, 896], P('stage', 'data')
- moment1_up: float32 [2, 896, 4864], P('stage', 'data')
- moment2_up: float32 [2, 896, 4864], P('stage', 'data')
- moment1_down: float32 [2, 4864, 896], P('stage', 'data')
- moment2_down: float32 [2, 4864, 896], P('stage', 'data')
- compute_up: bfloat16 [2, 896, 4864], P('stage')
- compute_down: bfloat16 [2, 4864, 896], P('stage')
- accum_up: float32 [4, 2, 896, 4864], P('data', 'stage')
- accum_down: float32 [4, 2, 4864, 896], P('data', 'stage')
- stage_acts: bfloat16 [2, 8192, 896], P('stage', 'data')
- loss_grad: bfloat16 [8192, 896], P('data')
- next_micro: bfloat16 [16, 8192, 896], P(None, 'data')
- learn_rate: float32 [], replicated
- max_norm: float32 [], replicated
Outputs:
- output 1: float32 [2, 896, 4864], P('stage', 'data')
- output 2: float32 [2, 4864, 896], P('stage', 'data')
- output 3: float32 [2, 896, 4864], P('stage', 'data')
- output 4: float32 [2, 896, 4864], P('stage', 'data')
- output 5: float32 [2, 4864, 896], P('stage', 'data')
- output 6: float32 [2, 4864, 896], P('stage', 'data')
- output 7: bfloat16 [16, 8192, 896], P(None, 'data')
All inputs are finite; a program needn't handle non-finite values.
Results may differ from a plain program's by a relative error of at most 0.00562341.
Values are sent between devices in bfloat16 or wider.
A program may use at most 1 GiB of HBM per device.

v0:
```python
import jax
import jax.numpy as jnp
from jax import lax
from jax.sharding import PartitionSpec as P

BETA_ONE = 0.9
BETA_TWO = 0.95
ADAM_EPS = 1e-8
WEIGHT_DECAY = 0.1
NORM_EPS = 1e-6
STEP_NUM = 10
BIAS_ONE = 1.0 - BETA_ONE ** STEP_NUM
BIAS_TWO = 1.0 - BETA_TWO ** STEP_NUM
DOT_ROWS = (((0,), (0,)), ((), ()))
DOT_COLS = (((1,), (1,)), ((), ()))


def gelu_tanh(pre_act):
    return jax.nn.gelu(pre_act, approximate=True)


def stage_forward(stage_in, w_up, w_down):
    pre_act = jnp.dot(stage_in, w_up, preferred_element_type=jnp.float32)
    hidden = gelu_tanh(pre_act).astype(jnp.bfloat16)
    branch = jnp.dot(hidden, w_down, preferred_element_type=jnp.float32)
    return (stage_in.astype(jnp.float32) + branch).astype(jnp.bfloat16)


def stage_backward(stage_in, grad_in, w_up, w_down):
    pre_act = jnp.dot(stage_in, w_up, preferred_element_type=jnp.float32)
    hidden, gelu_pull = jax.vjp(gelu_tanh, pre_act)
    hidden = hidden.astype(jnp.bfloat16)
    dw_down = lax.dot_general(hidden, grad_in, DOT_ROWS, preferred_element_type=jnp.float32)
    d_hidden = lax.dot_general(grad_in, w_down, DOT_COLS, preferred_element_type=jnp.float32)
    d_pre = gelu_pull(d_hidden)[0].astype(jnp.bfloat16)
    dw_up = lax.dot_general(stage_in, d_pre, DOT_ROWS, preferred_element_type=jnp.float32)
    d_in = grad_in.astype(jnp.float32) + lax.dot_general(d_pre, w_up, DOT_COLS, preferred_element_type=jnp.float32)
    return dw_up, dw_down, d_in.astype(jnp.bfloat16)


def adamw_update(master, moment_one, moment_two, grad_step, learn_rate):
    mom_one = BETA_ONE * moment_one + (1.0 - BETA_ONE) * grad_step
    mom_two = BETA_TWO * moment_two + (1.0 - BETA_TWO) * grad_step * grad_step
    step_dir = (mom_one / BIAS_ONE) / (jnp.sqrt(mom_two / BIAS_TWO) + ADAM_EPS)
    new_master = master - learn_rate * (step_dir + WEIGHT_DECAY * master)
    return new_master, mom_one, mom_two


def solution(mesh):
    n_stage = mesh.shape['stage']
    n_data = mesh.shape['data']
    last_stage = n_stage - 1
    back_perm = [(source, source - 1) for source in range(1, n_stage)]
    fwd_perm = [(source, source + 1) for source in range(last_stage)]

    def backward_stages(my_stage, stage_in, grad_last, w_up, w_down, acc_up, acc_down):
        def run_stage(operands):
            grad_in, sum_up, sum_down = operands
            dw_up, dw_down, d_in = stage_backward(stage_in, grad_in, w_up, w_down)
            return sum_up + dw_up, sum_down + dw_down, d_in

        def pass_through(operands):
            return operands[1], operands[2], operands[0]

        grad_buf = grad_last
        for step in range(n_stage):
            acc_up, acc_down, d_in = lax.cond(my_stage == last_stage - step, run_stage, pass_through,
                                              (grad_buf, acc_up, acc_down))
            if step < last_stage:
                grad_buf = lax.ppermute(d_in, 'stage', back_perm)
        return acc_up, acc_down

    def forward_stages(my_stage, micro_in, w_up, w_down):
        def run_block(block):
            return stage_forward(block, w_up, w_down)

        def keep_block(block):
            return block

        n_micro = micro_in.shape[0]
        n_steps = n_micro + last_stage
        received = jnp.zeros_like(micro_in[0])
        results = []
        for step in range(n_steps):
            stage_in = jnp.where(my_stage == 0, micro_in[min(step, n_micro - 1)], received)
            active = (my_stage <= step) & (my_stage > step - n_micro)
            stage_out = lax.cond(active, run_block, keep_block, stage_in)
            if step >= last_stage:
                results.append(stage_out)
            if step < n_steps - 1:
                received = lax.ppermute(stage_out, 'stage', fwd_perm)
        stacked = jnp.stack(results)
        own_part = jnp.where(my_stage == last_stage, stacked, jnp.zeros_like(stacked))
        return lax.psum(own_part, 'stage')

    def step_body(master_up, master_down, moment1_up, moment2_up, moment1_down, moment2_down,
                  compute_up, compute_down, accum_up, accum_down, stage_acts, loss_grad, next_micro,
                  learn_rate, max_norm):
        my_stage = lax.axis_index('stage')
        sum_up, sum_down = backward_stages(my_stage, stage_acts[0], loss_grad, compute_up[0], compute_down[0],
                                           accum_up[0, 0], accum_down[0, 0])
        shard_up = lax.psum_scatter(sum_up, 'data', scatter_dimension=0, tiled=True) / n_data
        shard_down = lax.psum_scatter(sum_down, 'data', scatter_dimension=0, tiled=True) / n_data
        local_sq = jnp.sum(shard_up * shard_up) + jnp.sum(shard_down * shard_down)
        total_sq = lax.psum(local_sq, ('stage', 'data'))
        clip = jnp.minimum(1.0, max_norm / (jnp.sqrt(total_sq) + NORM_EPS))
        new_up, mom1_up, mom2_up = adamw_update(master_up[0], moment1_up[0], moment2_up[0], clip * shard_up, learn_rate)
        new_down, mom1_down, mom2_down = adamw_update(master_down[0], moment1_down[0], moment2_down[0], clip * shard_down, learn_rate)
        full_up = lax.all_gather(new_up.astype(jnp.bfloat16), 'data', axis=0, tiled=True)
        full_down = lax.all_gather(new_down.astype(jnp.bfloat16), 'data', axis=0, tiled=True)
        last_acts = forward_stages(my_stage, next_micro, full_up, full_down)
        return (new_up[None], new_down[None], mom1_up[None], mom2_up[None],
                mom1_down[None], mom2_down[None], last_acts)

    shard_spec = P('stage', 'data', None)
    whole_spec = P('stage', None, None)
    accum_spec = P('data', 'stage', None, None)
    micro_spec = P(None, 'data', None)
    in_specs = (shard_spec,) * 6 + (whole_spec, whole_spec, accum_spec, accum_spec,
                                    P('stage', 'data', None), P('data', None), micro_spec, P(), P())
    out_specs = (shard_spec,) * 6 + (micro_spec,)
    return jax.shard_map(step_body, mesh=mesh, in_specs=in_specs, out_specs=out_specs, check_vma=False)
```

profile of v0, /device:TPU:0, one launch (start us, length us, event | category | flops | bytes accessed | tf_op | source)
XLA Modules:
  0.0 2502.7 jit_solution(1775678188854984927)
XLA Ops:
  49.5 170.4 %collective-permute-done = bf16[2048,896]{1,0:T(8,128)(2,1)} collective-permute-done((bf16[2048,896]{1,0:T(8,128)(2,1)}, bf16[2048,896]{1,0:T(8,128)(2,1)}, u32[]{:S(2)}, u32[]{:S(2)}) %collective-permute-start) | collective-permute-done | bytes 3670048 | tf_op jit(solution)/shard_map/ppermute | solution.py:70
  219.9 144.0 %conditional.20 = ((f32[896,4864]{0,1:T(8,128)}, f32[4864,896]{1,0:T(8,128)})) conditional(s32[]{:T(128)} %convert_element_type.234, (f32[896,4864]{0,1:T(8,128)}, f32[4864,896]{1,0:T(8,128)}) %tuple.188, (bf16[2048,896]{1,0:T(8,128)(2,1)}, bf16[4864,896]{1,0:T(8,128)(2,1)}, bf16[2048,896]{1,0:T(8,128)(2,1)}, bf16[896,4864]{1,0:T(8,128)(2,1)}, ...), branch_computations={%region_2.0_spmd, %region_3.0_spmd} | conditional | flops 71701430272 | bytes 261226528 | solution.py:67
  219.9 29.0 %fusion.273 = f32[2048,4864]{1,0:T(8,128)} fusion(bf16[2048,896]{1,0:T(8,128)(2,1)} %get-tuple-element.215, bf16[896,4864]{1,0:T(8,128)(2,1)} %get-tuple-element.216), kind=kOutput, calls=%fused_computation.356 | convolution fusion | flops 17850957824 | bytes 52232192 | tf_op jit(solution)/shard_map/cond/branch_1_fun/dot_general | solution.py:30
  248.9 46.7 %fusion.359 = bf16[2048,4864]{1,0:T(8,128)(2,1)} fusion(f32[2048,4864]{1,0:T(8,128)} %fusion.273, bf16[2048,896]{1,0:T(8,128)(2,1)} %get-tuple-element.213, bf16[4864,896]{1,0:T(8,128)(2,1)} %get-tuple-element.214), kind=kOutput, calls=%fused_computation.26.clone.clone.clone.clone.1 | convolution fusion | flops 18050187264 | bytes 72155136 | tf_op jit(solution)/shard_map/cond/branch_1_fun/dot_general | solution.py:34
  295.6 30.3 %bitcast_add_fusion.1 = f32[896,4864]{0,1:T(8,128)} fusion(f32[896,4864]{0,1:T(8,128)} %get-tuple-element.212, bf16[2048,896]{1,0:T(8,128)(2,1)} %get-tuple-element.215, bf16[2048,4864]{1,0:T(8,128)(2,1)} %fusion.359), kind=kOutput, calls=%fused_computation.30 | convolution fusion | flops 17855315968 | bytes 58458112 | tf_op jit(solution)/shard_map/cond/branch_1_fun/dot_general | solution.py:36
  325.8 37.7 %fusion.27 = f32[4864,896]{1,0:T(8,128)} fusion(f32[4864,896]{1,0:T(8,128)} %get-tuple-element.217, bf16[2048,896]{1,0:T(8,128)(2,1)} %get-tuple-element.213, f32[2048,4864]{1,0:T(8,128)} %fusion.273), kind=kOutput, calls=%fused_computation.32 | convolution fusion | flops 17944969216 | bytes 78381056 | tf_op jit(solution)/shard_map/cond/branch_1_fun/dot_general | solution.py:33
  384.3 154.0 %reduce-scatter.3.cloned.1.call-done = f32[224,4864]{1,0:T(8,128)} async-done(((f32[896,4864]{1,0:T(8,128)}), f32[224,4864]{1,0:T(8,128)}) %reduce-scatter.3.cloned.1.call-update) | async-done | bytes 4358160 | tf_op jit(solution)/shard_map/reduce_scatter | solution.py:102
  542.3 152.6 %reduce-scatter.5.cloned.1.call-done = f32[1216,896]{1,0:T(8,128)} async-done(((f32[4864,896]{1,0:T(8,128)}), f32[1216,896]{1,0:T(8,128)}) %reduce-scatter.5.cloned.1.call-update) | async-done | bytes 4358160 | tf_op jit(solution)/shard_map/reduce_scatter | solution.py:103
  753.2 69.9 %all-gather.3.cloned.1.call-done = bf16[896,4864]{1,0:T(8,128)(2,1)} async-done(((bf16[224,4864]{1,0:T(8,128)(2,1)}), bf16[896,4864]{1,0:T(8,128)(2,1)}) %all-gather.3.cloned.1.call-update) | async-done | bytes 8716304 | tf_op jit(solution)/shard_map/all_gather | solution.py:109
  823.1 86.3 %all-gather.5.cloned.1.call-done = bf16[4864,896]{1,0:T(8,128)(2,1)} async-done(((bf16[1216,896]{1,0:T(8,128)(2,1)}), bf16[4864,896]{1,0:T(8,128)(2,1)}) %all-gather.5.cloned.1.call-update) | async-done | bytes 8716304 | tf_op jit(solution)/shard_map/all_gather | solution.py:110
  909.4 58.6 %conditional.21 = (bf16[2048,896]{1,0:T(8,128)(2,1)}) conditional(s32[]{:T(128)} %convert_element_type.237, bf16[2048,896]{1,0:T(8,128)(2,1)} %select_bitcast_fusion, (bf16[2048,896]{1,0:T(8,128)(2,1)}, bf16[896,4864]{1,0:T(8,128)(2,1)}, bf16[4864,896]{1,0:T(8,128)(2,1)}) %tuple.190), branch_computations={%region_9.10_spmd, %region_10.11_spmd} | conditional | flops 35797073920 | bytes 103153704 | solution.py:87
  909.6 33.4 %fusion.45.clone.6 = bf16[2048,4864]{1,0:T(8,128)(2,1)} fusion(bf16[2048,896]{1,0:T(8,128)(2,1)} %get-tuple-element.218, bf16[896,4864]{1,0:T(8,128)(2,1)} %get-tuple-element.219), kind=kOutput, calls=%fused_computation.51.clone.clone.clone.clone.clone.1 | convolution fusion | flops 17940611072 | bytes 32309248 | tf_op jit(solution)/shard_map/cond/branch_1_fun/dot_general | solution.py:23
  979.8 66.4 %conditional.22 = (bf16[2048,896]{1,0:T(8,128)(2,1)}, bf16[1,2048,896]{2,1,0:T(8,128)(2,1)}) conditional(s32[]{:T(128)} %convert_element_type.236, bf16[2048,896]{1,0:T(8,128)(2,1)} %bitcast_select_fusion.15, (bf16[2048,896]{1,0:T(8,128)(2,1)}, bf16[896,4864]{1,0:T(8,128)(2,1)S(1)}, bf16[4864,896]{1,0:T(8,128)(2,1)}) %tuple.276), branch_computations={%region_11.12_spmd, %region_12.13_spmd} | conditional | flops 35797073920 | bytes 75628560 | solution.py:87
  979.8 34.7 %fusion.58.clone.4 = bf16[2048,4864]{1,0:T(8,128)(2,1)} fusion(bf16[2048,896]{1,0:T(8,128)(2,1)} %get-tuple-element.221, bf16[896,4864]{1,0:T(8,128)(2,1)S(1)} %get-tuple-element.222), kind=kOutput, calls=%fused_computation.66.clone.clone.clone.clone.clone | convolution fusion | flops 17940611072 | bytes 32309248 | tf_op jit(solution)/shard_map/cond/branch_1_fun/dot_general | solution.py:23
  1014.5 27.5 %add_convert_fusion.2 = bf16[2048,896]{1,0:T(8,128)(2,1)} fusion(bf16[2048,896]{1,0:T(8,128)(2,1)} %get-tuple-element.221, bf16[4864,896]{1,0:T(8,128)(2,1)} %get-tuple-element.223, bf16[2048,4864]{1,0:T(8,128)(2,1)} %fusion.58.clone.4), kind=kOutput, calls=%fused_computation.68 | convolution fusion | flops 17856462848 | bytes 35979264 | tf_op jit(solution)/shard_map/cond/branch_1_fun/dot_general | solution.py:25
  1060.2 62.4 %conditional.23 = (bf16[2048,896]{1,0:T(8,128)(2,1)}, bf16[1,2048,896]{2,1,0:T(8,128)(2,1)}) conditional(s32[]{:T(128)} %convert_element_type.240, bf16[2048,896]{1,0:T(8,128)(2,1)} %bitcast_select_fusion.14, (bf16[2048,896]{1,0:T(8,128)(2,1)}, bf16[896,4864]{1,0:T(8,128)(2,1)}, bf16[4864,896]{1,0:T(8,128)(2,1)S(1)}) %tuple.284), branch_computations={%region_13.14_spmd, %region_14.15_spmd} | conditional | flops 35797073920 | bytes 75628560 | solution.py:87
  1060.2 33.2 %fusion.71.clone.4 = bf16[2048,4864]{1,0:T(8,128)(2,1)} fusion(bf16[2048,896]{1,0:T(8,128)(2,1)} %get-tuple-element.224, bf16[896,4864]{1,0:T(8,128)(2,1)} %get-tuple-element.225), kind=kOutput, calls=%fused_computation.81.clone.clone.clone.clone.clone | convolution fusion | flops 17940611072 | bytes 32309248 | tf_op jit(solution)/shard_map/cond/branch_1_fun/dot_general | solution.py:23
  1136.6 66.4 %conditional.24 = (bf16[2048,896]{1,0:T(8,128)(2,1)}, bf16[1,2048,896]{2,1,0:T(8,128)(2,1)}) conditional(s32[]{:T(128)} %convert_element_type.241, bf16[2048,896]{1,0:T(8,128)(2,1)} %bitcast_select_fusion.13, (bf16[2048,896]{1,0:T(8,128)(2,1)}, bf16[896,4864]{1,0:T(8,128)(2,1)S(1)}, bf16[4864,896]{1,0:T(8,128)(2,1)}) %tuple.277), branch_computations={%region_15.16_spmd, %region_16.17_spmd} | conditional | flops 35797073920 | bytes 75628560 | solution.py:87
  1136.6 34.7 %fusion.84.clone.4 = bf16[2048,4864]{1,0:T(8,128)(2,1)} fusion(bf16[2048,896]{1,0:T(8,128)(2,1)} %get-tuple-element.227, bf16[896,4864]{1,0:T(8,128)(2,1)S(1)} %get-tuple-element.228), kind=kOutput, calls=%fused_computation.96.clone.clone.clone.clone.clone | convolution fusion | flops 17940611072 | bytes 32309248 | tf_op jit(solution)/shard_map/cond/branch_1_fun/dot_general | solution.py:23
  1171.3 27.5 %add_convert_fusion.4 = bf16[2048,896]{1,0:T(8,128)(2,1)} fusion(bf16[2048,896]{1,0:T(8,128)(2,1)} %get-tuple-element.227, bf16[4864,896]{1,0:T(8,128)(2,1)} %get-tuple-element.229, bf16[2048,4864]{1,0:T(8,128)(2,1)} %fusion.84.clone.4), kind=kOutput, calls=%fused_computation.98 | convolution fusion | flops 17856462848 | bytes 35979264 | tf_op jit(solution)/shard_map/cond/branch_1_fun/dot_general | solution.py:25
  1217.0 62.4 %conditional.25 = (bf16[2048,896]{1,0:T(8,128)(2,1)}, bf16[1,2048,896]{2,1,0:T(8,128)(2,1)}) conditional(s32[]{:T(128)} %convert_element_type.242, bf16[2048,896]{1,0:T(8,128)(2,1)} %bitcast_select_fusion.12, (bf16[2048,896]{1,0:T(8,128)(2,1)}, bf16[896,4864]{1,0:T(8,128)(2,1)}, bf16[4864,896]{1,0:T(8,128)(2,1)S(1)}) %tuple.285), branch_computations={%region_17.18_spmd, %region_18.19_spmd} | conditional | flops 35797073920 | bytes 75628560 | solution.py:87
  1217.0 33.2 %fusion.97.clone.4 = bf16[2048,4864]{1,0:T(8,128)(2,1)} fusion(bf16[2048,896]{1,0:T(8,128)(2,1)} %get-tuple-element.230, bf16[896,4864]{1,0:T(8,128)(2,1)} %get-tuple-element.231), kind=kOutput, calls=%fused_computation.111.clone.clone.clone.clone.clone | convolution fusion | flops 17940611072 | bytes 32309248 | tf_op jit(solution)/shard_map/cond/branch_1_fun/dot_general | solution.py:23
  1293.4 66.4 %conditional.26 = (bf16[2048,896]{1,0:T(8,128)(2,1)}, bf16[1,2048,896]{2,1,0:T(8,128)(2,1)}) conditional(s32[]{:T(128)} %convert_element_type.243, bf16[2048,896]{1,0:T(8,128)(2,1)} %bitcast_select_fusion.11, (bf16[2048,896]{1,0:T(8,128)(2,1)}, bf16[896,4864]{1,0:T(8,128)(2,1)S(1)}, bf16[4864,896]{1,0:T(8,128)(2,1)}) %tuple.278), branch_computations={%region_19.20_spmd, %region_20.21_spmd} | conditional | flops 35797073920 | bytes 75628560 | solution.py:87
  1293.4 34.7 %fusion.110.clone.4 = bf16[2048,4864]{1,0:T(8,128)(2,1)} fusion(bf16[2048,896]{1,0:T(8,128)(2,1)} %get-tuple-element.233, bf16[896,4864]{1,0:T(8,128)(2,1)S(1)} %get-tuple-element.234), kind=kOutput, calls=%fused_computation.126.clone.clone.clone.clone.clone | convolution fusion | flops 17940611072 | bytes 32309248 | tf_op jit(solution)/shard_map/cond/branch_1_fun/dot_general | solution.py:23
  1373.7 62.4 %conditional.27 = (bf16[2048,896]{1,0:T(8,128)(2,1)}, bf16[1,2048,896]{2,1,0:T(8,128)(2,1)}) conditional(s32[]{:T(128)} %convert_element_type.244, bf16[2048,896]{1,0:T(8,128)(2,1)} %bitcast_select_fusion.10, (bf16[2048,896]{1,0:T(8,128)(2,1)}, bf16[896,4864]{1,0:T(8,128)(2,1)}, bf16[4864,896]{1,0:T(8,128)(2,1)S(1)}) %tuple.286), branch_computations={%region_21.22_spmd, %region_22.23_spmd} | conditional | flops 35797073920 | bytes 75628560 | solution.py:87
  1373.7 33.2 %fusion.123.clone.4 = bf16[2048,4864]{1,0:T(8,128)(2,1)} fusion(bf16[2048,896]{1,0:T(8,128)(2,1)} %get-tuple-element.236, bf16[896,4864]{1,0:T(8,128)(2,1)} %get-tuple-element.237), kind=kOutput, calls=%fused_computation.141.clone.clone.clone.clone.clone | convolution fusion | flops 17940611072 | bytes 32309248 | tf_op jit(solution)/shard_map/cond/branch_1_fun/dot_general | solution.py:23
  1450.1 66.4 %conditional.28 = (bf16[2048,896]{1,0:T(8,128)(2,1)}, bf16[1,2048,896]{2,1,0:T(8,128)(2,1)}) conditional(s32[]{:T(128)} %convert_element_type.245, bf16[2048,896]{1,0:T(8,128)(2,1)} %bitcast_select_fusion.9, (bf16[2048,896]{1,0:T(8,128)(2,1)}, bf16[896,4864]{1,0:T(8,128)(2,1)S(1)}, bf16[4864,896]{1,0:T(8,128)(2,1)}) %tuple.279), branch_computations={%region_23.24_spmd, %region_24.25_spmd} | conditional | flops 35797073920 | bytes 75628560 | solution.py:87
  1450.1 34.7 %fusion.136.clone.4 = bf16[2048,4864]{1,0:T(8,128)(2,1)} fusion(bf16[2048,896]{1,0:T(8,128)(2,1)} %get-tuple-element.239, bf16[896,4864]{1,0:T(8,128)(2,1)S(1)} %get-tuple-element.240), kind=kOutput, calls=%fused_computation.156.clone.clone.clone.clone.clone | convolution fusion | flops 17940611072 | bytes 32309248 | tf_op jit(solution)/shard_map/cond/branch_1_fun/dot_general | solution.py:23
  1484.8 27.5 %add_convert_fusion.8 = bf16[2048,896]{1,0:T(8,128)(2,1)} fusion(bf16[2048,896]{1,0:T(8,128)(2,1)} %get-tuple-element.239, bf16[4864,896]{1,0:T(8,128)(2,1)} %get-tuple-element.241, bf16[2048,4864]{1,0:T(8,128)(2,1)} %fusion.136.clone.4), kind=kOutput, calls=%fused_computation.158 | convolution fusion | flops 17856462848 | bytes 35979264 | tf_op jit(solution)/shard_map/cond/branch_1_fun/dot_general | solution.py:25
  1530.5 62.4 %conditional.29 = (bf16[2048,896]{1,0:T(8,128)(2,1)}, bf16[1,2048,896]{2,1,0:T(8,128)(2,1)}) conditional(s32[]{:T(128)} %convert_element_type.246, bf16[2048,896]{1,0:T(8,128)(2,1)} %bitcast_select_fusion.8, (bf16[2048,896]{1,0:T(8,128)(2,1)}, bf16[896,4864]{1,0:T(8,128)(2,1)}, bf16[4864,896]{1,0:T(8,128)(2,1)S(1)}) %tuple.287), branch_computations={%region_25.26_spmd, %region_26.27_spmd} | conditional | flops 35797073920 | bytes 75628560 | solution.py:87
  1530.5 33.2 %fusion.149.clone.4 = bf16[2048,4864]{1,0:T(8,128)(2,1)} fusion(bf16[2048,896]{1,0:T(8,128)(2,1)} %get-tuple-element.242, bf16[896,4864]{1,0:T(8,128)(2,1)} %get-tuple-element.243), kind=kOutput, calls=%fused_computation.171.clone.clone.clone.clone.clone | convolution fusion | flops 17940611072 | bytes 32309248 | tf_op jit(solution)/shard_map/cond/branch_1_fun/dot_general | solution.py:23
  1606.9 66.5 %conditional.30 = (bf16[2048,896]{1,0:T(8,128)(2,1)}, bf16[1,2048,896]{2,1,0:T(8,128)(2,1)}) conditional(s32[]{:T(128)} %convert_element_type.247, bf16[2048,896]{1,0:T(8,128)(2,1)} %bitcast_select_fusion.7, (bf16[2048,896]{1,0:T(8,128)(2,1)}, bf16[896,4864]{1,0:T(8,128)(2,1)S(1)}, bf16[4864,896]{1,0:T(8,128)(2,1)}) %tuple.280), branch_computations={%region_27.28_spmd, %region_28.29_spmd} | conditional | flops 35797073920 | bytes 75628560 | solution.py:87
  1606.9 34.7 %fusion.162.clone.4 = bf16[2048,4864]{1,0:T(8,128)(2,1)} fusion(bf16[2048,896]{1,0:T(8,128)(2,1)} %get-tuple-element.245, bf16[896,4864]{1,0:T(8,128)(2,1)S(1)} %get-tuple-element.246), kind=kOutput, calls=%fused_computation.186.clone.clone.clone.clone.clone | convolution fusion | flops 17940611072 | bytes 32309248 | tf_op jit(solution)/shard_map/cond/branch_1_fun/dot_general | solution.py:23
  1641.5 27.5 %add_convert_fusion.10 = bf16[2048,896]{1,0:T(8,128)(2,1)} fusion(bf16[2048,896]{1,0:T(8,128)(2,1)} %get-tuple-element.245, bf16[4864,896]{1,0:T(8,128)(2,1)} %get-tuple-element.247, bf16[2048,4864]{1,0:T(8,128)(2,1)} %fusion.162.clone.4), kind=kOutput, calls=%fused_computation.188 | convolution fusion | flops 17856462848 | bytes 35979264 | tf_op jit(solution)/shard_map/cond/branch_1_fun/dot_general | solution.py:25
  1687.3 62.4 %conditional.31 = (bf16[2048,896]{1,0:T(8,128)(2,1)}, bf16[1,2048,896]{2,1,0:T(8,128)(2,1)}) conditional(s32[]{:T(128)} %convert_element_type.248, bf16[2048,896]{1,0:T(8,128)(2,1)} %bitcast_select_fusion.6, (bf16[2048,896]{1,0:T(8,128)(2,1)}, bf16[896,4864]{1,0:T(8,128)(2,1)}, bf16[4864,896]{1,0:T(8,128)(2,1)S(1)}) %tuple.288), branch_computations={%region_29.30_spmd, %region_30.31_spmd} | conditional | flops 35797073920 | bytes 75628560 | solution.py:87
  1687.3 33.2 %fusion.175.clone.4 = bf16[2048,4864]{1,0:T(8,128)(2,1)} fusion(bf16[2048,896]{1,0:T(8,128)(2,1)} %get-tuple-element.248, bf16[896,4864]{1,0:T(8,128)(2,1)} %get-tuple-element.249), kind=kOutput, calls=%fused_computation.201.clone.clone.clone.clone.clone | convolution fusion | flops 17940611072 | bytes 32309248 | tf_op jit(solution)/shard_map/cond/branch_1_fun/dot_general | solution.py:23
  1763.7 66.4 %conditional.32 = (bf16[2048,896]{1,0:T(8,128)(2,1)}, bf16[1,2048,896]{2,1,0:T(8,128)(2,1)}) conditional(s32[]{:T(128)} %convert_element_type.249, bf16[2048,896]{1,0:T(8,128)(2,1)} %bitcast_select_fusion.5, (bf16[2048,896]{1,0:T(8,128)(2,1)}, bf16[896,4864]{1,0:T(8,128)(2,1)S(1)}, bf16[4864,896]{1,0:T(8,128)(2,1)}) %tuple.281), branch_computations={%region_31.32_spmd, %region_32.33_spmd} | conditional | flops 35797073920 | bytes 75628560 | solution.py:87
  1763.7 34.7 %fusion.188.clone.4 = bf16[2048,4864]{1,0:T(8,128)(2,1)} fusion(bf16[2048,896]{1,0:T(8,128)(2,1)} %get-tuple-element.251, bf16[896,4864]{1,0:T(8,128)(2,1)S(1)} %get-tuple-element.252), kind=kOutput, calls=%fused_computation.216.clone.clone.clone.clone.clone | convolution fusion | flops 17940611072 | bytes 32309248 | tf_op jit(solution)/shard_map/cond/branch_1_fun/dot_general | solution.py:23
  1844.1 62.4 %conditional.33 = (bf16[2048,896]{1,0:T(8,128)(2,1)}, bf16[1,2048,896]{2,1,0:T(8,128)(2,1)}) conditional(s32[]{:T(128)} %convert_element_type.250, bf16[2048,896]{1,0:T(8,128)(2,1)} %bitcast_select_fusion.4, (bf16[2048,896]{1,0:T(8,128)(2,1)}, bf16[896,4864]{1,0:T(8,128)(2,1)}, bf16[4864,896]{1,0:T(8,128)(2,1)S(1)}) %tuple.289), branch_computations={%region_33.34_spmd, %region_34.35_spmd} | conditional | flops 35797073920 | bytes 75628560 | solution.py:87
  1844.1 33.2 %fusion.201.clone.4 = bf16[2048,4864]{1,0:T(8,128)(2,1)} fusion(bf16[2048,896]{1,0:T(8,128)(2,1)} %get-tuple-element.254, bf16[896,4864]{1,0:T(8,128)(2,1)} %get-tuple-element.255), kind=kOutput, calls=%fused_computation.231.clone.clone.clone.clone.clone | convolution fusion | flops 17940611072 | bytes 32309248 | tf_op jit(solution)/shard_map/cond/branch_1_fun/dot_general | solution.py:23
  1920.5 66.4 %conditional.34 = (bf16[2048,896]{1,0:T(8,128)(2,1)}, bf16[1,2048,896]{2,1,0:T(8,128)(2,1)}) conditional(s32[]{:T(128)} %convert_element_type.251, bf16[2048,896]{1,0:T(8,128)(2,1)} %bitcast_select_fusion.3, (bf16[2048,896]{1,0:T(8,128)(2,1)}, bf16[896,4864]{1,0:T(8,128)(2,1)S(1)}, bf16[4864,896]{1,0:T(8,128)(2,1)}) %tuple.282), branch_computations={%region_35.36_spmd, %region_36.37_spmd} | conditional | flops 35797073920 | bytes 75628560 | solution.py:87
  1920.5 34.7 %fusion.214.clone.4 = bf16[2048,4864]{1,0:T(8,128)(2,1)} fusion(bf16[2048,896]{1,0:T(8,128)(2,1)} %get-tuple-element.257, bf16[896,4864]{1,0:T(8,128)(2,1)S(1)} %get-tuple-element.258), kind=kOutput, calls=%fused_computation.246.clone.clone.clone.clone.clone | convolution fusion | flops 17940611072 | bytes 32309248 | tf_op jit(solution)/shard_map/cond/branch_1_fun/dot_general | solution.py:23
  2000.8 62.6 %conditional.35 = (bf16[2048,896]{1,0:T(8,128)(2,1)}, bf16[1,2048,896]{2,1,0:T(8,128)(2,1)}) conditional(s32[]{:T(128)} %convert_element_type.252, bf16[2048,896]{1,0:T(8,128)(2,1)} %bitcast_select_fusion.2, (bf16[2048,896]{1,0:T(8,128)(2,1)}, bf16[896,4864]{1,0:T(8,128)(2,1)}, bf16[4864,896]{1,0:T(8,128)(2,1)S(1)}) %tuple.290), branch_computations={%region_37.38_spmd, %region_38.39_spmd} | conditional | flops 35797073920 | bytes 75628560 | solution.py:87
  2000.8 33.2 %fusion.227.clone.4 = bf16[2048,4864]{1,0:T(8,128)(2,1)} fusion(bf16[2048,896]{1,0:T(8,128)(2,1)} %get-tuple-element.260, bf16[896,4864]{1,0:T(8,128)(2,1)} %get-tuple-element.261), kind=kOutput, calls=%fused_computation.261.clone.clone.clone.clone.clone | convolution fusion | flops 17940611072 | bytes 32309248 | tf_op jit(solution)/shard_map/cond/branch_1_fun/dot_general | solution.py:23
  2084.5 54.4 %conditional.36 = (bf16[2048,896]{1,0:T(8,128)(2,1)S(1)}, bf16[1,2048,896]{2,1,0:T(8,128)(2,1)S(1)}) conditional(s32[]{:T(128)} %convert_element_type.253, bf16[2048,896]{1,0:T(8,128)(2,1)S(1)} %bitcast_select_fusion.1, (bf16[2048,896]{1,0:T(8,128)(2,1)S(1)}, bf16[896,4864]{1,0:T(8,128)(2,1)S(1)}, bf16[4864,896]{1,0:T(8,128)(2,1)}) %tuple.283), branch_computations={%region_39.40_spmd, %region_40.41_spmd} | conditional | flops 35797073920 | bytes 75628560 | solution.py:87
  2084.5 27.5 %fusion.240.clone.4 = bf16[2048,4864]{1,0:T(8,128)(2,1)} fusion(bf16[2048,896]{1,0:T(8,128)(2,1)S(1)} %get-tuple-element.263, bf16[896,4864]{1,0:T(8,128)(2,1)S(1)} %get-tuple-element.264), kind=kOutput, calls=%fused_computation.276.clone.clone.clone.clone.clone | convolution fusion | flops 17940611072 | bytes 32309248 | tf_op jit(solution)/shard_map/cond/branch_1_fun/dot_general | solution.py:23
  2215.9 240.0 %all-reduce.2.cloned.1.call-done = bf16[16,2048,896]{2,1,0:T(8,128)(2,1)} async-done(((bf16[16,2048,896]{2,1,0:T(8,128)(2,1)}), bf16[16,2048,896]{2,1,0:T(8,128)(2,1)}) %all-reduce.2.cloned.1.call-update) | async-done | bytes 58720272 | tf_op jit(solution)/shard_map/psum | solution.py:94
  2455.9 39.9 %copy.121 = bf16[16,2048,896]{2,1,0:T(8,128)(2,1)} copy(bf16[16,2048,896]{2,1,0:T(8,128)(2,1)} %all-reduce.2.cloned.1.call-done) | data formatting | bytes 117440512
  (154 shorter events, 781.0 us)
Async XLA Ops:
  7.2 531.2 %reduce-scatter.3.cloned.1.call-start = ((), (), s32[]{:S(2)}) async-start(), calls=%async_computation.2 | async-start | bytes 21790720 | tf_op jit(solution)/shard_map/reduce_scatter | solution.py:102
  7.2 12.0 copy-start
  48.2 171.7 %collective-permute-start = (bf16[2048,896]{1,0:T(8,128)(2,1)}, bf16[2048,896]{1,0:T(8,128)(2,1)}, u32[]{:S(2)}, u32[]{:S(2)}) collective-permute-start(bf16[2048,896]{1,0:T(8,128)(2,1)} %get-tuple-element.313), channel_id=1, source_target_pairs={{1,0},{3,2},{5,4},{7,6}} | collective-permute-start | bytes 11010056 | tf_op jit(solution)/shard_map/ppermute | solution.py:70
  382.9 312.1 %reduce-scatter.5.cloned.1.call-start = ((), (), s32[]{:S(2)}) async-start(), calls=%async_computation.3 | async-start | bytes 21790720 | tf_op jit(solution)/shard_map/reduce_scatter | solution.py:103
  383.6 439.5 %all-gather.3.cloned.1.call-start = ((), (), s32[]{:S(2)}) async-start(), calls=%async_computation.4 | async-start | bytes 10895360 | tf_op jit(solution)/shard_map/all_gather | solution.py:109
  736.3 173.0 %all-gather.5.cloned.1.call-start = ((), (), s32[]{:S(2)}) async-start(), calls=%async_computation.5 | async-start | bytes 10895360 | tf_op jit(solution)/shard_map/all_gather | solution.py:110
  749.0 1706.9 %all-reduce.2.cloned.1.call-start = ((), (), s32[]{:S(2)}) async-start(), calls=%async_computation.6 | async-start | bytes 117440512 | tf_op jit(solution)/shard_map/psum | solution.py:94
  909.5 33.4 %copy-start.15 = (bf16[4864,896]{1,0:T(8,128)(2,1)S(1)}, bf16[4864,896]{1,0:T(8,128)(2,1)}, u32[]{:S(2)}) copy-start(bf16[4864,896]{1,0:T(8,128)(2,1)} %get-tuple-element.220) | copy-start | bytes 26148868 | tf_op jit(solution)/shard_map/cond
  968.0 7.6 collective-permute-start.1
  971.2 8.6 copy-start.1
  1046.2 9.8 collective-permute-start.2
  1051.8 8.4 copy-start.8
  1122.6 9.7 collective-permute-start.3
  1128.0 8.6 copy-start.2
  1203.0 9.8 collective-permute-start.4
  1208.4 8.6 copy-start.9
  1279.4 9.8 collective-permute-start.5
  1285.0 8.4 copy-start.3
  1359.7 9.7 collective-permute-start.6
  1365.1 8.6 copy-start.10
  1436.1 9.8 collective-permute-start.7
  1441.5 8.6 copy-start.4
  1516.5 9.8 collective-permute-start.8
  1522.1 8.4 copy-start.11
  1592.9 9.8 collective-permute-start.9
  1598.2 8.6 copy-start.5
  1673.3 9.8 collective-permute-start.10
  1678.7 8.6 copy-start.12
  1749.7 9.7 collective-permute-start.11
  1755.3 8.4 copy-start.6
  1830.1 9.7 collective-permute-start.12
  1835.5 8.6 copy-start.13
  1906.5 9.7 collective-permute-start.13
  1911.9 8.6 copy-start.7
  1986.8 9.8 collective-permute-start.14
  1992.4 8.4 copy-start.14
  2063.4 18.1 collective-permute-start.15
  2077.1 7.3 slice-start
  2077.1 7.3 slice-start.1
  2081.5 3.0 slice-start.2
  2138.9 49.5 %collective-permute-start.16 = (bf16[2048,896]{1,0:T(8,128)(2,1)S(1)}, bf16[2048,896]{1,0:T(8,128)(2,1)S(1)}, u32[]{:S(2)}, u32[]{:S(2)}) collective-permute-start(bf16[2048,896]{1,0:T(8,128)(2,1)S(1)} %get-tuple-element.345), channel_id=1, source_target_pairs={{0,1},{2,3},{4,5},{6,7}} | collective-permute-start | bytes 11010056 | tf_op jit(solution)/shard_map/ppermute | solution.py:91
Sparse Core Ops, SparseCore 0:
  383.0 155.3 reduce-scatter.2
  541.4 153.4 reduce-scatter.4
  736.5 86.5 all-gather.2
  824.7 84.6 all-gather.4
  2216.0 239.8 all-reduce.1
where the time goes:
time: 2510 us; the launch traced here: 2500 us
  matrix products  1100 us (44%)
  waiting for transfers between devices  934 us (37%)
  local copies, waits for them, and re-layouts  215 us (9%)
  other arithmetic  123 us (5%)
  starting transfers between devices  82.5 us (3%)
    dot_general x16, matrix products, stage_forward(): pre_act = jnp.dot(stage_in, w_up, preferred_element_type=jnp.float32)  536 us
    dot_general x16, matrix products, stage_forward(): branch = jnp.dot(hidden, w_down, preferred_element_type=jnp.float32)  420 us
    psum x1, waiting for transfers between devices, forward_stages(): return lax.psum(own_part, 'stage')  240 us
    ppermute x1, waiting for transfers between devices, backward_stages(): grad_buf = lax.ppermute(d_in, 'stage', back_perm)  170 us
    reduce_scatter x1, waiting for transfers between devices, step_body(): lax.psum_scatter(sum_up, 'data', scatter_dimension=0, tiled=True) / n_data  154 us
    reduce_scatter x1, waiting for transfers between devices, step_body(): lax.psum_scatter(sum_down, 'data', scatter_dimension=0, tiled=True) / n_data  153 us
    unnamed x55, local copies, waits for them, and re-layouts  133 us
    all_gather x1, waiting for transfers between devices, step_body(): lax.all_gather(new_down.astype(jnp.bfloat16), 'data', axis=0, tiled=True)  86.3 us
  transfers between devices with their start and end apart: 22, of which 20 were waited for; matrix products, arithmetic and copies ran while one was open for 3% of the time, Pallas kernels for 0%

commit v1 on v0

v1 whole, which is shorter than its diff:
```python
import functools

import jax
import jax.numpy as jnp
from jax import lax
from jax.experimental import pallas as pl
from jax.experimental.pallas import tpu as pltpu
from jax.sharding import PartitionSpec as P

BETA_ONE = 0.9
BETA_TWO = 0.95
ADAM_EPS = 1e-8
WEIGHT_DECAY = 0.1
NORM_EPS = 1e-6
STEP_NUM = 10
BIAS_ONE = 1.0 - BETA_ONE ** STEP_NUM
BIAS_TWO = 1.0 - BETA_TWO ** STEP_NUM
DOT_ROWS = (((0,), (0,)), ((), ()))
DOT_COLS = (((1,), (1,)), ((), ()))

D_MODEL = 896
FF_WIDTH = 4864
TOKENS = 2048
N_DATA = 4
UP_ROWS = D_MODEL // N_DATA
DOWN_ROWS = FF_WIDTH // N_DATA
GELU_A = 0.7978845608028654
GELU_B = GELU_A * 0.044715
FWD_ROWS = 512
FWD_CHUNKS = (1280, 1280, 1280, 1024)
BACK_CHUNK = 256
VMEM_LIMIT = 63 * 1024 * 1024


def gelu_tanh(u):
    half = 0.5 * u
    return half + half * jnp.tanh(u * (GELU_A + GELU_B * (u * u)))


def gelu_slope(u):
    sq = u * u
    t = jnp.tanh(u * (GELU_A + GELU_B * sq))
    return 0.5 * (1.0 + t) + (0.5 * u) * (1.0 - t * t) * (GELU_A + (3.0 * GELU_B) * sq)


def dot32(a, b, dims=(((1,), (0,)), ((), ()))):
    return lax.dot_general(a, b, dims, preferred_element_type=jnp.float32)


def adamw_update(master, moment_one, moment_two, grad_step, learn_rate):
    mom_one = BETA_ONE * moment_one + (1.0 - BETA_ONE) * grad_step
    mom_two = BETA_TWO * moment_two + (1.0 - BETA_TWO) * grad_step * grad_step
    step_dir = (mom_one / BIAS_ONE) / (jnp.sqrt(mom_two / BIAS_TWO) + ADAM_EPS)
    new_master = master - learn_rate * (step_dir + WEIGHT_DECAY * master)
    return new_master, mom_one, mom_two


def back_one_kernel(acts_ref, grad_ref, up_ref, down_ref, pre_ref, hid_ref, din_ref, total):
    step = pl.program_id(0)

    @pl.when(step == 0)
    def _():
        total[...] = grad_ref[...].astype(jnp.float32)

    for r in range(0, TOKENS, 512):
        rows = pl.ds(r, 512)
        u = dot32(acts_ref[rows, :], up_ref[...])
        pre_ref[rows, :] = u
        hid_ref[rows, :] = gelu_tanh(u).astype(jnp.bfloat16)
        d_hid = dot32(grad_ref[rows, :], down_ref[...], DOT_COLS)
        d_pre = (d_hid * gelu_slope(u)).astype(jnp.bfloat16)
        total[rows, :] += dot32(d_pre, up_ref[...], DOT_COLS)

    @pl.when(step == pl.num_programs(0) - 1)
    def _():
        din_ref[...] = total[...].astype(jnp.bfloat16)


def back_one(acts, grad, w_up, w_down):
    steps = FF_WIDTH // BACK_CHUNK
    whole = pl.BlockSpec((TOKENS, D_MODEL), lambda j: (0, 0))
    cols = pl.BlockSpec((TOKENS, BACK_CHUNK), lambda j: (0, j))
    return pl.pallas_call(
        back_one_kernel,
        grid=(steps,),
        in_specs=[whole, whole, pl.BlockSpec((D_MODEL, BACK_CHUNK), lambda j: (0, j)),
                  pl.BlockSpec((BACK_CHUNK, D_MODEL), lambda j: (j, 0))],
        out_specs=[cols, cols, whole],
        out_shape=[jax.ShapeDtypeStruct((TOKENS, FF_WIDTH), jnp.float32),
                   jax.ShapeDtypeStruct((TOKENS, FF_WIDTH), jnp.bfloat16),
                   jax.ShapeDtypeStruct((TOKENS, D_MODEL), jnp.bfloat16)],
        scratch_shapes=[pltpu.VMEM((TOKENS, D_MODEL), jnp.float32)],
        compiler_params=pltpu.CompilerParams(vmem_limit_bytes=VMEM_LIMIT),
        cost_estimate=pl.CostEstimate(flops=6 * TOKENS * D_MODEL * FF_WIDTH, bytes_accessed=90_000_000, transcendentals=0),
        name='back_one',
    )(acts, grad, w_up, w_down)


def weight_copies(block, up_ref, down_ref, w1, w2, sem):
    found = []
    for d in range(N_DATA):
        found.append(pltpu.make_async_copy(up_ref.at[d, block], w1.at[block, pl.ds(d * UP_ROWS, UP_ROWS)], sem.at[block, d]))
        if down_ref is not None:
            found.append(pltpu.make_async_copy(down_ref.at[d, block], w2.at[block, pl.ds(d * DOWN_ROWS, DOWN_ROWS)], sem.at[block, N_DATA + d]))
    return found


def hidden_kernel(stage_ref, x_ref, up_ref, hid_ref, w1, sem):
    @pl.when(pl.program_id(0) == 0)
    def _():
        copies = weight_copies(0, up_ref, None, w1, None, sem)
        for c in copies:
            c.start()
        for c in copies:
            c.wait()

    off = 0
    for width in FWD_CHUNKS:
        u = dot32(x_ref[0], w1[0, :, off:off + width])
        hid_ref[0, :, off:off + width] = gelu_tanh(u).astype(jnp.bfloat16)
        off += width


def forward_kernel(has_hidden, *refs):
    refs = list(refs)
    _, x_ref = refs[:2]
    hid_ref = refs[2] if has_hidden else None
    up_ref, down_ref, out_ref, send_ref, w1, w2, sem = refs[-7:]
    step = pl.program_id(0)

    @pl.when(step == 0)
    def _():
        for block in range(2):
            for c in weight_copies(block, up_ref, down_ref, w1, w2, sem):
                c.start()

    x = x_ref[0]
    for block in range(2):
        @pl.when(step == 0)
        def _():
            for c in weight_copies(block, up_ref, down_ref, w1, w2, sem):
                c.wait()

        total = x.astype(jnp.float32)
        off = 0
        for width in FWD_CHUNKS:
            if block == 0 and has_hidden:
                h = hid_ref[0, :, off:off + width]
            else:
                h = gelu_tanh(dot32(x, w1[block, :, off:off + width])).astype(jnp.bfloat16)
            total = total + dot32(h, w2[block, off:off + width, :])
            off += width
        x = total.astype(jnp.bfloat16)
    send_ref[0] = x
    out_ref[0] = x


def own_spec(micro_per, start):
    row_blocks = TOKENS // FWD_ROWS
    return pl.BlockSpec((1, FWD_ROWS, D_MODEL),
                        lambda i, st: (st[0] * micro_per + start + i // row_blocks, i % row_blocks, 0))


def hidden_call(stage, micro, full_up, start, count):
    row_blocks = TOKENS // FWD_ROWS
    return pl.pallas_call(
        hidden_kernel,
        grid_spec=pltpu.PrefetchScalarGridSpec(
            num_scalar_prefetch=1, grid=(count * row_blocks,),
            in_specs=[own_spec(micro.shape[0] // 2, start), pl.BlockSpec(memory_space=pl.ANY)],
            out_specs=pl.BlockSpec((1, FWD_ROWS, FF_WIDTH), lambda i, st: (i // row_blocks, i % row_blocks, 0)),
            scratch_shapes=[pltpu.VMEM((1, D_MODEL, FF_WIDTH), jnp.bfloat16), pltpu.SemaphoreType.DMA((1, N_DATA))]),
        out_shape=jax.ShapeDtypeStruct((count, TOKENS, FF_WIDTH), jnp.bfloat16),
        compiler_params=pltpu.CompilerParams(vmem_limit_bytes=VMEM_LIMIT),
        cost_estimate=pl.CostEstimate(flops=2 * count * TOKENS * D_MODEL * FF_WIDTH, bytes_accessed=count * 24_000_000, transcendentals=0),
        name='hidden_call',
    )(stage, micro, full_up)


def forward_call(stage, micro, full_up, full_down, start, count, hidden=None, into=None):
    row_blocks = TOKENS // FWD_ROWS
    spec = own_spec(micro.shape[0] // 2, start)
    any_spec = pl.BlockSpec(memory_space=pl.ANY)
    args, in_specs = [stage, micro], [spec]
    if hidden is not None:
        args.append(hidden)
        in_specs.append(pl.BlockSpec((1, FWD_ROWS, FF_WIDTH), lambda i, st: (i // row_blocks, i % row_blocks, 0)))
    aliases = {}
    if into is not None:
        aliases = {len(args): 0}
        args.append(into)
        in_specs.append(any_spec)
    args += [full_up, full_down]
    in_specs += [any_spec, any_spec]
    return pl.pallas_call(
        functools.partial(forward_kernel, hidden is not None),
        grid_spec=pltpu.PrefetchScalarGridSpec(
            num_scalar_prefetch=1, grid=(count * row_blocks,),
            in_specs=in_specs,
            out_specs=[spec, pl.BlockSpec((1, FWD_ROWS, D_MODEL), lambda i, st: (i // row_blocks, i % row_blocks, 0))],
            scratch_shapes=[pltpu.VMEM((2, D_MODEL, FF_WIDTH), jnp.bfloat16), pltpu.VMEM((2, FF_WIDTH, D_MODEL), jnp.bfloat16),
                            pltpu.SemaphoreType.DMA((2, 2 * N_DATA))]),
        out_shape=[jax.ShapeDtypeStruct(micro.shape, jnp.bfloat16),
                   jax.ShapeDtypeStruct((count, TOKENS, D_MODEL), jnp.bfloat16)],
        input_output_aliases=aliases,
        compiler_params=pltpu.CompilerParams(vmem_limit_bytes=VMEM_LIMIT),
        cost_estimate=pl.CostEstimate(flops=8 * count * TOKENS * D_MODEL * FF_WIDTH, bytes_accessed=count * 30_000_000, transcendentals=0),
        name='forward_call',
    )(*args)


def solution(mesh):
    n_data = mesh.shape['data']

    def step_body(master_up, master_down, moment1_up, moment2_up, moment1_down, moment2_down,
                  compute_up, compute_down, accum_up, accum_down, stage_acts, loss_grad, next_micro,
                  learn_rate, max_norm):
        my_stage = lax.axis_index('stage')
        stage = my_stage.astype(jnp.int32)[None]
        acts, w_up, w_down = stage_acts[0], compute_up[0], compute_down[0]

        pre_act, hidden, d_in = back_one(acts, loss_grad, w_up, w_down)
        below = lax.ppermute(d_in, 'stage', [(1, 0)])
        grad_in = jnp.where(my_stage == 1, loss_grad, below)
        sum_down = accum_down[0, 0] + dot32(hidden, grad_in, DOT_ROWS)
        sum_down, grad_in = lax.optimization_barrier((sum_down, grad_in))
        shard_down = lax.psum_scatter(sum_down, 'data', scatter_dimension=0, tiled=True) / n_data
        d_hid = dot32(grad_in, w_down, DOT_COLS)
        d_pre = (d_hid * gelu_slope(pre_act)).astype(jnp.bfloat16)
        sum_up = accum_up[0, 0] + dot32(acts, d_pre, DOT_ROWS)
        shard_up = lax.psum_scatter(sum_up, 'data', scatter_dimension=0, tiled=True) / n_data

        local_sq = jnp.sum(shard_up * shard_up) + jnp.sum(shard_down * shard_down)
        total_sq = lax.psum(local_sq, ('stage', 'data'))
        clip = jnp.minimum(1.0, max_norm / (jnp.sqrt(total_sq) + NORM_EPS))
        new_up, mom1_up, mom2_up = adamw_update(master_up[0], moment1_up[0], moment2_up[0], clip * shard_up, learn_rate)
        full_up = lax.all_gather(new_up.astype(jnp.bfloat16), ('data', 'stage'))
        full_up = full_up.reshape(N_DATA, 2, UP_ROWS, FF_WIDTH)
        new_down, mom1_down, mom2_down = adamw_update(master_down[0], moment1_down[0], moment2_down[0], clip * shard_down, learn_rate)
        full_down = lax.all_gather(new_down.astype(jnp.bfloat16), ('data', 'stage'))
        full_down = full_down.reshape(N_DATA, 2, DOWN_ROWS, D_MODEL)

        half = next_micro.shape[0] // 2
        swap = [(0, 1), (1, 0)]
        hid = hidden_call(stage, next_micro, full_up, 0, 4)
        out, sent_a = forward_call(stage, next_micro, full_up, full_down, 0, 4, hidden=hid)
        got_a = lax.ppermute(sent_a, 'stage', swap)
        out, sent_b = forward_call(stage, next_micro, full_up, full_down, 4, 3, into=out)
        got_b = lax.ppermute(sent_b, 'stage', swap)
        out, sent_c = forward_call(stage, next_micro, full_up, full_down, 7, 1, into=out)
        got_c = lax.ppermute(sent_c, 'stage', swap)
        other = (1 - my_stage) * half
        out = lax.dynamic_update_slice(out, got_a, (other, 0, 0))
        out = lax.dynamic_update_slice(out, got_b, (other + 4, 0, 0))
        last_acts = lax.dynamic_update_slice(out, got_c, (other + 7, 0, 0))
        return (new_up[None], new_down[None], mom1_up[None], mom2_up[None],
                mom1_down[None], mom2_down[None], last_acts)

    shard_spec = P('stage', 'data', None)
    whole_spec = P('stage', None, None)
    accum_spec = P('data', 'stage', None, None)
    micro_spec = P(None, 'data', None)
    in_specs = (shard_spec,) * 6 + (whole_spec, whole_spec, accum_spec, accum_spec,
                                    P('stage', 'data', None), P('data', None), micro_spec, P(), P())
    out_specs = (shard_spec,) * 6 + (micro_spec,)
    return jax.shard_map(step_body, mesh=mesh, in_specs=in_specs, out_specs=out_specs, check_vma=False)
```

time: 2510 us -> 1510 us (0.60)
  matrix products: 1100 us -> 101 us
  Pallas kernels: 0 us -> 847 us
  waiting for transfers between devices: 934 us -> 369 us
  local copies, waits for them, and re-layouts: 215 us -> 109 us
  other arithmetic: 123 us -> 37.6 us
  starting transfers between devices: 82.5 us -> 2.52 us
    dot_general x36 -> x3, matrix products: 1100 us -> 101 us  [dot32(): return lax.dot_general(a, b, dims, preferred_element_type=jnp.float32)]
    pallas_call x0 -> x5, Pallas kernels: none -> 847 us  [the longest x3 644 us: forward_call(): pl.pallas_call(functools.partial(forward_kernel, hidden is not None), gri...]
    psum x1 -> x0, waiting for transfers between devices: 240 us -> none  [forward_stages(): return lax.psum(own_part, 'stage')]
    ppermute x17 -> x4, waiting for transfers between devices: 230 us -> 0.01 us  [the longest x1 0.01 us: step_body(): below = lax.ppermute(d_in, 'stage', [(1, 0)])]
    reduce_scatter x1 -> x0, waiting for transfers between devices: 154 us -> none  [step_body(): lax.psum_scatter(sum_up, 'data', scatter_dimension=0, tiled=True) / n_data]
    unnamed x5, waiting for transfers between devices: 0.76 us -> 146 us
    select_n x18 -> x1, other arithmetic: 89.6 us -> 2.43 us  [step_body(): grad_in = jnp.where(my_stage == 1, loss_grad, below)]
    ppermute x17 -> x4, starting transfers between devices: 82.3 us -> 2.36 us  [the longest x1 1.54 us: step_body(): below = lax.ppermute(d_in, 'stage', [(1, 0)])]
  transfers between devices with their start and end apart: 22 -> 8, of which waited for: 20 -> 3; matrix products, arithmetic and copies ran while one was open for 3% -> 6% of each run, Pallas kernels for 0% -> 32%
where the time goes in v1:
time: 1510 us
  Pallas kernels  847 us (56%)
  waiting for transfers between devices  369 us (24%)
  local copies, waits for them, and re-layouts  109 us (7%)
  matrix products  101 us (7%)
  other arithmetic  37.6 us (2%)
  blocking collectives  22.4 us (1%)
  between operations  17.3 us (1%)
    pallas_call x3, Pallas kernels, forward_call(): pl.pallas_call(functools.partial(forward_kernel, hidden is not None), gri...  644 us
    unnamed x5, waiting for transfers between devices  146 us
    reduce_scatter x1, waiting for transfers between devices, step_body(): lax.psum_scatter(sum_down, 'data', scatter_dimension=0, tiled=True) / n_data  146 us
    pallas_call x1, Pallas kernels, hidden_call(): pl.pallas_call(hidden_kernel, grid_spec=pltpu.PrefetchScalarGridSpec(num_...  111 us
    dot_general x3, matrix products, dot32(): return lax.dot_general(a, b, dims, preferred_element_type=jnp.float32)  101 us
    pallas_call x1, Pallas kernels, back_one(): pl.pallas_call(back_one_kernel, grid=(steps,), in_specs=[whole, whole, pl...  92.9 us
    unnamed x11, local copies, waits for them, and re-layouts  79.1 us
    all_gather x1, waiting for transfers between devices, step_body(): full_up = lax.all_gather(new_up.astype(jnp.bfloat16), ('data', 'stage'))  76.4 us
  transfers between devices with their start and end apart: 8, of which 3 were waited for; matrix products, arithmetic and copies ran while one was open for 6% of the time, Pallas kernels for 32%

profile of v1, /device:TPU:0, one launch (start us, length us, event | category | flops | bytes accessed | tf_op | source)
XLA Modules:
  0.0 1505.3 jit_solution(4677901833268359053)
XLA Ops:
  7.2 0.0 reduce-scatter.7.cloned.1.call-start
  7.2 92.9 %back_one.1 = (f32[2048,4864]{1,0:T(8,128)}, bf16[2048,4864]{1,0:T(8,128)(2,1)}, bf16[2048,896]{1,0:T(8,128)(2,1)}) custom-call(bf16[2048,896]{1,0:T(8,128)(2,1)} %bitcast.100, bf16[2048,896]{1,0:T(8,128)(2,1)} %grad_ref.1, bf16[896,4864]{1,0:T(8,128)(2,1)} %bitcast.98, bf16[4864,896]{1,0:T(8,128)(2,1)} %bitcast.99), custom_call_target="tpu_custom_call" | custom-call | flops 53552873472 | bytes 90000000 | tf_op jit(solution)/shard_map/back_one/pallas_call | solution.py:83
  100.1 1.5 collective-permute-start
  101.7 18.9 %copy.34 = f32[1,1,896,4864]{2,3,1,0:T(8,128)} copy(f32[1,1,896,4864]{3,2,1,0:T(8,128)} %param.23) | data formatting | bytes 34865152 | tf_op args[8]
  120.6 0.0 collective-permute-done
  120.6 2.4 broadcast_select_fusion
  123.0 0.0 copy-start
  123.1 1.8 copy-done
  124.9 29.0 %bitcast_add_fusion.1 = f32[4864,896]{1,0:T(8,128)} fusion(f32[1,1,4864,896]{3,2,1,0:T(8,128)} %param.24, bf16[2048,4864]{1,0:T(8,128)(2,1)} %get-tuple-element.18, bf16[2048,896]{1,0:T(8,128)(2,1)S(1)} %broadcast_select_fusion), kind=kOutput, calls=%fused_computation.2 | convolution fusion | flops 17855315968 | bytes 58458112 | tf_op jit(solution)/shard_map/dot_general | solution.py:47
  153.9 40.9 %multiply_convert_fusion.clone.4 = bf16[2048,4864]{1,0:T(8,128)(2,1)} fusion(f32[2048,4864]{1,0:T(8,128)} %get-tuple-element.21, bf16[2048,896]{1,0:T(8,128)(2,1)} %copy-done, bf16[1,4864,896]{2,1,0:T(8,128)(2,1)} %param.22), kind=kOutput, calls=%fused_computation.clone.clone.clone.1 | convolution fusion | flops 18010341376 | bytes 72155136 | tf_op jit(solution)/shard_map/dot_general | solution.py:47
  194.8 30.6 %bitcast_add_fusion = f32[896,4864]{0,1:T(8,128)} fusion(f32[1,1,896,4864]{2,3,1,0:T(8,128)} %copy.34, bf16[1,2048,896]{2,1,0:T(8,128)(2,1)} %param.25, bf16[2048,4864]{1,0:T(8,128)(2,1)} %multiply_convert_fusion.clone.4), kind=kOutput, calls=%fused_computation.1 | convolution fusion | flops 17855315968 | bytes 58458112 | tf_op jit(solution)/shard_map/dot_general | solution.py:47
  225.5 18.9 %copy.40 = f32[896,4864]{1,0:T(8,128)} copy(f32[896,4864]{0,1:T(8,128)} %bitcast_add_fusion) | data formatting | bytes 34865152
  244.4 0.0 reduce-scatter.7.cloned.1.call-update
  244.4 0.0 reduce-scatter.5.cloned.1.call-start
  244.5 0.7 reduce-scatter.5.cloned.1.call-update
  245.2 0.0 all-gather.5.cloned.1.call-start
  245.2 5.6 copy.35
  251.5 5.7 copy.33
  257.8 145.6 %reduce-scatter.7.cloned.1.call-done = f32[224,4864]{1,0:T(8,128)} async-done(((f32[896,4864]{1,0:T(8,128)}), f32[224,4864]{1,0:T(8,128)}) %reduce-scatter.7.cloned.1.call-update) | async-done | bytes 4358160
  403.4 5.7 copy.41
  409.1 5.0 multiply_reduce_fusion
  414.1 145.9 %reduce-scatter.5.cloned.1.call-done = f32[1216,896]{1,0:T(8,128)} async-done(((f32[4864,896]{1,0:T(8,128)}), f32[1216,896]{1,0:T(8,128)}) %reduce-scatter.5.cloned.1.call-update) | async-done | bytes 4358160 | tf_op jit(solution)/shard_map/reduce_scatter | solution.py:227
  560.1 4.0 multiply_reduce_fusion.1
  565.3 5.6 copy.32
  571.0 22.4 %psum.7 = f32[]{:T(128)} all-reduce(f32[]{:T(128)S(6)} %add.85), channel_id=1, replica_groups=mesh['data'=4,'stage'=2] {'stage','data'}, use_global_device_ids=true, to_apply=%region_4.5 | all-reduce | flops 1 | bytes 8 | tf_op jit(solution)/shard_map/psum | solution.py:234
  594.1 13.6 fusion.19
  607.7 2.9 copy.36
  610.6 0.0 all-gather.5.cloned.1.call-update
  610.7 0.0 all-gather.7.cloned.1.call-start
  610.7 12.6 fusion.18
  623.3 0.0 all-gather.7.cloned.1.call-update
  623.3 76.4 %all-gather.5.cloned.1.call-done = bf16[1792,4864]{1,0:T(8,128)(2,1)} async-done(((bf16[224,4864]{1,0:T(8,128)(2,1)}), bf16[1792,4864]{1,0:T(8,128)(2,1)}) %all-gather.5.cloned.1.call-update) | async-done | bytes 17432592 | tf_op jit(solution)/shard_map/all_gather | solution.py:237
  699.7 110.9 %hidden_call.1.refs_2_ = bf16[4,2048,4864]{2,1,0:T(8,128)(2,1)} custom-call(s32[1]{0:T(128)} %bitcast.18.stage_ref.refs_0_, bf16[16,2048,896]{2,1,0:T(8,128)(2,1)} %refs_1_.5, bf16[4,2,224,4864]{3,2,1,0:T(8,128)(2,1)} %bitcast.91), custom_call_target="tpu_custom_call" | custom-call | flops 71403831296 | bytes 96000000 | tf_op jit(solution)/shard_map/hidden_call/pallas_call | solution.py:166
  810.6 0.0 all-gather.7.cloned.1.call-done
  810.6 276.2 %forward_call.3 = (bf16[16,2048,896]{2,1,0:T(8,128)(2,1)}, bf16[4,2048,896]{2,1,0:T(8,128)(2,1)}) custom-call(s32[1]{0:T(128)} %bitcast.18.stage_ref.refs_0_, bf16[16,2048,896]{2,1,0:T(8,128)(2,1)} %refs_1_.5, bf16[4,2048,4864]{2,1,0:T(8,128)(2,1)} %hidden_call.1.refs_2_, bf16[4,2,224,4864]{3,2,1,0:T(8,128)(2,1)} %bitcast.92, bf16[4,2,1216,896]{3,2,1,0:T(8,128)(2,1)} %bitcast.95), custom_call_target="tpu_custom_call" | custom-call | flops 285615325184 | bytes 120000000 | tf_op jit(solution)/shard_map/forward_call/pallas_call | solution.py:195
  1086.8 0.3 collective-permute-start.1
  1087.0 271.0 %forward_call.4 = (bf16[16,2048,896]{2,1,0:T(8,128)(2,1)}, bf16[3,2048,896]{2,1,0:T(8,128)(2,1)}) custom-call(s32[1]{0:T(128)} %bitcast.18.stage_ref.refs_0_, bf16[16,2048,896]{2,1,0:T(8,128)(2,1)} %refs_1_.5, bf16[16,2048,896]{2,1,0:T(8,128)(2,1)} %get-tuple-element.23.refs_2_, bf16[4,2,224,4864]{3,2,1,0:T(8,128)(2,1)} %bitcast.93, ...), custom_call_target="tpu_custom_call", output_to_operand_aliasing={{0}: (2, {})} | custom-call | flops 214211493888 | bytes 90000000 | tf_op jit(solution)/shard_map/forward_call/pallas_call | solution.py:195
  1358.1 0.3 collective-permute-start.2
  1358.3 96.4 %forward_call.5 = (bf16[16,2048,896]{2,1,0:T(8,128)(2,1)}, bf16[1,2048,896]{2,1,0:T(8,128)(2,1)}) custom-call(s32[1]{0:T(128)} %bitcast.18.stage_ref.refs_0_, bf16[16,2048,896]{2,1,0:T(8,128)(2,1)} %refs_1_.5, bf16[16,2048,896]{2,1,0:T(8,128)(2,1)} %get-tuple-element.24.refs_2_, bf16[4,2,224,4864]{3,2,1,0:T(8,128)(2,1)} %bitcast.94, ...), custom_call_target="tpu_custom_call", output_to_operand_aliasing={{0}: (2, {})} | custom-call | flops 71403831296 | bytes 30000000 | tf_op jit(solution)/shard_map/forward_call/pallas_call | solution.py:195
  1454.7 0.3 collective-permute-start.3
  1455.0 5.6 copy.37
  1460.6 5.6 copy.38
  1466.2 5.6 copy.39
  1471.8 0.0 collective-permute-done.1
  1471.8 13.1 constant_dynamic-update-slice_fusion.2
  1484.9 9.6 constant_dynamic-update-slice_fusion.1
  1494.5 0.0 collective-permute-done.3
  1494.5 4.2 constant_dynamic-update-slice_fusion
  (1 shorter events, 0.0 us)
Async XLA Ops:
  7.2 396.3 %reduce-scatter.7.cloned.1.call-start = ((), (), s32[]{:S(2)}) async-start(), calls=%async_computation.5 | async-start | bytes 21790720
  100.1 20.5 %collective-permute-start = (bf16[2048,896]{1,0:T(8,128)(2,1)}, bf16[2048,896]{1,0:T(8,128)(2,1)}, u32[]{:S(2)}, u32[]{:S(2)}) collective-permute-start(bf16[2048,896]{1,0:T(8,128)(2,1)} %get-tuple-element.19), channel_id=1, source_target_pairs={{1,0},{3,2},{5,4},{7,6}} | collective-permute-start | bytes 11010056 | tf_op jit(solution)/shard_map/ppermute | solution.py:223
  123.0 1.8 copy-start
  244.4 315.6 %reduce-scatter.5.cloned.1.call-start = ((), (), s32[]{:S(2)}) async-start(), calls=%async_computation.2 | async-start | bytes 21790720 | tf_op jit(solution)/shard_map/reduce_scatter | solution.py:227
  245.2 454.5 %all-gather.5.cloned.1.call-start = ((), (), s32[]{:S(2)}) async-start(), calls=%async_computation.3 | async-start | bytes 19611648 | tf_op jit(solution)/shard_map/all_gather | solution.py:237
  610.7 199.9 %all-gather.7.cloned.1.call-start = ((), (), s32[]{:S(2)}) async-start(), calls=%async_computation.4 | async-start | bytes 19611648 | tf_op jit(solution)/shard_map/all_gather | solution.py:240
  1086.8 385.0 %collective-permute-start.1 = (bf16[4,2048,896]{2,1,0:T(8,128)(2,1)}, bf16[4,2048,896]{2,1,0:T(8,128)(2,1)}, u32[]{:S(2)}, u32[]{:S(2)}) collective-permute-start(bf16[4,2048,896]{2,1,0:T(8,128)(2,1)} %get-tuple-element.26), channel_id=1, source_target_pairs={{0,1},{1,0},{2,3},{3,2},{4,5},{5,4},{6,7},{7,6}} | collective-permute-start | bytes 44040200 | tf_op jit(solution)/shard_map/ppermute | solution.py:247
  1358.1 126.8 %collective-permute-start.2 = (bf16[3,2048,896]{2,1,0:T(8,128)(2,1)}, bf16[3,2048,896]{2,1,0:T(8,128)(2,1)}, u32[]{:S(2)}, u32[]{:S(2)}) collective-permute-start(bf16[3,2048,896]{2,1,0:T(8,128)(2,1)} %get-tuple-element.27), channel_id=1, source_target_pairs={{0,1},{1,0},{2,3},{3,2},{4,5},{5,4},{6,7},{7,6}} | collective-permute-start | bytes 33030152 | tf_op jit(solution)/shard_map/ppermute | solution.py:249
  1454.7 39.8 %collective-permute-start.3 = (bf16[1,2048,896]{2,1,0:T(8,128)(2,1)}, bf16[1,2048,896]{2,1,0:T(8,128)(2,1)}, u32[]{:S(2)}, u32[]{:S(2)}) collective-permute-start(bf16[1,2048,896]{2,1,0:T(8,128)(2,1)} %get-tuple-element.28), channel_id=1, source_target_pairs={{0,1},{1,0},{2,3},{3,2},{4,5},{5,4},{6,7},{7,6}} | collective-permute-start | bytes 11010056 | tf_op jit(solution)/shard_map/ppermute | solution.py:251
Sparse Core Ops, SparseCore 0:
  244.5 158.8 reduce-scatter.6
  406.5 153.4 reduce-scatter.4
  610.8 88.8 all-gather.4
  701.9 86.9 all-gather.6
